TPU v7x, 32 devices: a whole 2x2x4 slice. The times are simulated.
32 devices in a mesh: section: 2 (over x), tensor: 4 (over z), dp: 4 (over y, core).
Axes of the slice: x: 2, y: 2, z: 4, core: 2. Of those that a mesh axis runs over, the one named last changes fastest.
Arguments:
- tokens: bfloat16 [16, 4096], P(None, ('section', 'dp')), may hold values from -100 to 100
- attn_gain: float32 [4096], P(('section', 'dp')), may hold values from 0.1 to 1.9
- qkv_weight: bfloat16 [4096, 10240], P(('section', 'dp'), 'tensor'), may hold values from -0.09375 to 0.09375
- qkv_order: int32 [10], replicated, may hold values from 0 to 9, each once
- cache_keys: bfloat16 [16, 8, 4096, 128], P(('section', 'dp'), 'tensor'), may hold values from -1300 to 1300
- cache_values: bfloat16 [16, 8, 4096, 128], P(('section', 'dp'), 'tensor'), may hold values from -6 to 6
- cache_len: int32 [16], P(('section', 'dp')), may hold values from 2 to 4096, as said below
- out_weight: bfloat16 [8192, 4096], P('tensor', ('section', 'dp')), may hold values from -0.0625 to 0.0625
- ffn_gain: float32 [4096], P(('section', 'dp')), may hold values from 0.1 to 1.9
- gate_up: bfloat16 [2, 4096, 28672], P(None, ('section', 'dp'), 'tensor'), may hold values from -0.09375 to 0.09375
- down_weight: bfloat16 [28672, 4096], P('tensor', ('section', 'dp')), may hold values from -0.03125 to 0.03125
Outputs:
- layer_out: bfloat16 [16, 4096], P(None, ('section', 'dp'))
Inputs may be any that keep to these rules, and one draw needn't show every extreme that they name: qkv_order is a permutation of 0 to 9, the same for every key-value group. `cache_len`: at least one sequence has all 4096 positions valid.
All inputs are finite; a program needn't handle non-finite values.
Results may differ from a plain program's by a relative error of at most 0.0065.
Values may be sent and summed in bfloat16 or wider, within the bound.
A program may use at most 64 MiB of HBM per device.

v0:
```python
import jax
import jax.numpy as jnp
from jax import lax
from jax.sharding import PartitionSpec as P

D = 4096
HEADS = 64
KV_HEADS = 8
HD = 128
LEN = 4096
GROUP = 10


def normalize(stream, gain_vec):
    wide = stream.astype(jnp.float32)
    squares = lax.psum(jnp.sum(wide * wide, axis=1), ("section", "dp"))
    factor = lax.rsqrt(squares / D + 1e-05)
    return (wide * factor[:, None] * gain_vec[None, :]).astype(jnp.bfloat16)


def rotate(vector, cosine, sine_part):
    half_dim = vector.shape[-1] // 2
    first_half = vector[..., :half_dim]
    second = vector[..., half_dim:]
    return jnp.concatenate(
        [first_half * cosine - second * sine_part, second * cosine + first_half * sine_part],
        axis=-1,
    )


def project_rows(row_block, weight_cols):
    return jnp.dot(
        lax.all_gather(row_block, ("section", "dp"), axis=0, tiled=True),
        weight_cols,
        preferred_element_type=jnp.float32,
    )


def add_residual(base_rows, partial_sum):
    summed = lax.psum(partial_sum, "tensor")
    return (base_rows.astype(jnp.float32) + summed).astype(jnp.bfloat16)


def body(
    tokens,
    attn_gain,
    qkv_weight,
    qkv_order,
    cache_keys,
    cache_values,
    cache_len,
    out_weight,
    ffn_gain,
    gate_up,
    down_weight,
):
    seq_count = cache_len.shape[0]
    local_groups = cache_keys.shape[1]
    per_group = HEADS // KV_HEADS
    normed = normalize(tokens, attn_gain)
    row_block = normed
    joined_cols = lax.psum_scatter(
        jnp.dot(row_block, qkv_weight, preferred_element_type=jnp.float32),
        ("section", "dp"),
        scatter_dimension=0,
        tiled=True,
    )
    blocks = joined_cols.reshape(seq_count, local_groups, GROUP, HD)
    onehot = (qkv_order[:, None] == jnp.arange(GROUP, dtype=jnp.int32)[None, :]).astype(jnp.float32)
    logical = jnp.einsum("bgjd,ji->bgid", blocks, onehot, precision=lax.Precision.HIGHEST)
    half_dim = HD // 2
    inv_freq = 500000.0 ** (-(2.0 * jnp.arange(half_dim, dtype=jnp.float32)) / HD)
    angles = cache_len.astype(jnp.float32)[:, None] * inv_freq[None, :]
    cosine = jnp.cos(angles)
    sine_part = jnp.sin(angles)
    queries = rotate(
        logical[:, :, :per_group], cosine[:, None, None, :], sine_part[:, None, None, :]
    ).astype(jnp.bfloat16)
    new_key = rotate(logical[:, :, per_group], cosine[:, None, :], sine_part[:, None, :]).astype(
        jnp.bfloat16
    )
    new_value = logical[:, :, per_group + 1].astype(jnp.bfloat16)
    inv_scale = 1.0 / jnp.sqrt(jnp.float32(HD))
    scores = (
        jnp.einsum("bgpd,bgld->bgpl", queries, cache_keys, preferred_element_type=jnp.float32)
        * inv_scale
    )
    own_score = (
        jnp.einsum("bgpd,bgd->bgp", queries, new_key, preferred_element_type=jnp.float32)
        * inv_scale
    )
    valid_mask = jnp.arange(LEN, dtype=jnp.int32)[None, :] < cache_len[:, None]
    masked = jnp.where(valid_mask[:, None, None, :], scores, -jnp.inf)
    peak = jnp.maximum(jnp.max(masked, axis=-1), own_score)
    weights = jnp.exp(masked - peak[..., None])
    own_weight = jnp.exp(own_score - peak)
    denom_sum = jnp.sum(weights, axis=-1) + own_weight
    probabilities = (weights / denom_sum[..., None]).astype(jnp.bfloat16)
    own_prob = (own_weight / denom_sum).astype(jnp.bfloat16)
    mixed_heads = jnp.einsum(
        "bgpl,bgld->bgpd", probabilities, cache_values, preferred_element_type=jnp.float32
    )
    mixed_heads = (
        mixed_heads
        + own_prob.astype(jnp.float32)[..., None] * new_value.astype(jnp.float32)[:, :, None, :]
    )
    attended = mixed_heads.astype(jnp.bfloat16).reshape(seq_count, -1)
    hidden_state = add_residual(tokens, project_rows(attended, out_weight))
    ffn_normed = normalize(hidden_state, ffn_gain)
    row_block = ffn_normed
    gate_and_up = lax.psum_scatter(
        jnp.einsum("rd,kdf->rkf", row_block, gate_up, preferred_element_type=jnp.float32),
        ("section", "dp"),
        scatter_dimension=0,
        tiled=True,
    )
    activated = (jax.nn.silu(gate_and_up[:, 0]) * gate_and_up[:, 1]).astype(jnp.bfloat16)
    return add_residual(hidden_state, project_rows(activated, down_weight))


def solution(mesh):
    return jax.shard_map(
        body,
        mesh=mesh,
        in_specs=(
            P(None, ("section", "dp")),
            P(("section", "dp")),
            P(("section", "dp"), "tensor"),
            P(),
            P(("section", "dp"), "tensor", None, None),
            P(("section", "dp"), "tensor", None, None),
            P(("section", "dp")),
            P("tensor", ("section", "dp")),
            P(("section", "dp")),
            P(None, ("section", "dp"), "tensor"),
            P("tensor", ("section", "dp")),
        ),
        out_specs=P(None, ("section", "dp")),
        check_vma=False,
    )
```

profile of v0, /device:TPU:0, one launch (start us, length us, event | category | flops | bytes accessed | tf_op | source)
XLA Modules:
  0.0 227.4 jit_solution(6629242835967836412)
XLA Ops:
  6.5 1.0 fusion.7
  7.5 15.1 %psum.28 = f32[16]{0:T(128)S(1)} all-reduce(f32[16]{0:T(128)S(1)} %fusion.7), channel_id=1, replica_groups=mesh['section'=2,'tensor'=4,'dp'=4] {'section','dp'}, use_global_device_ids=true, to_apply=%region_1.0 | all-reduce | flops 16 | bytes 128 | tf_op jit(solution)/shard_map/psum | solution.py:16
  22.7 1.9 fusion.19
  24.6 0.7 convert_element_type.47
  25.3 0.7 iota_compare_fusion
  26.2 1.2 dynamic-slice
  28.1 48.3 %all-reduce.5.cloned.1.call-done = f32[16,2560]{1,0:T(8,128)} async-done(((f32[16,2560]{1,0:T(8,128)}), f32[16,2560]{1,0:T(8,128)}) %all-reduce.5.cloned.1.call-update) | async-done | bytes 163856
  76.4 0.9 constant_dynamic-slice_fusion
  77.3 0.9 convolution_bitcast_fusion
  78.5 0.2 fusion.29
  78.7 3.5 %fusion.36 = (f32[2,2,8]{2,1,0:T(2,128)S(1)}, f32[2,2,8,4096]{3,2,1,0:T(8,128)S(1)}) fusion(bf16[2,2,4096,128]{3,2,1,0:T(8,128)(2,1)} %param.15, bf16[2,2,8,64]{3,2,1,0:T(8,128)(2,1)S(1)} %get-tuple-element.8, bf16[2,2,8,64]{3,2,1,0:T(8,128)(2,1)S(1)} %get-tuple-element.7, pred[2,4096]{1,0:T(4,128)(4,1)S(1)} %iota_compare_fusion), kind=kOutput, calls=%fused_computation.64 | convolution fusion | flops 33964000 | bytes 4735104 | tf_op jit(solution)/shard_map/bgpd,bgld->bgpl/dot_general | solution.py:85
  82.3 0.2 fusion.2
  82.5 0.7 fusion.1
  83.3 10.0 %all-gather = bf16[8,2,2048]{2,1,0:T(2,128)(2,1)S(1)} all-gather(bf16[1,2,2048]{2,1,0:T(2,128)(2,1)S(1)} %reshape.129), channel_id=1, replica_groups=mesh['section'=2,'tensor'=4,'dp'=4] {'section','dp'}, dimensions={0}, use_global_device_ids=true | all-gather | bytes 73728 | tf_op jit(solution)/shard_map/all_gather | solution.py:33
  93.3 2.0 fusion.37
  95.3 19.0 %psum.29 = f32[16,512]{1,0:T(8,128)S(1)} all-reduce(f32[16,512]{1,0:T(8,128)S(1)} %fusion.37), channel_id=1, replica_groups=mesh['section'=2,'tensor'=4,'dp'=4] {'tensor'}, use_global_device_ids=true, to_apply=%region_5.6 | all-reduce | flops 8192 | bytes 65536 | tf_op jit(solution)/shard_map/psum | solution.py:40
  114.4 11.8 %psum.30 = f32[16]{0:T(128)S(1)} all-reduce(f32[16]{0:T(128)S(1)} %get-tuple-element.5), channel_id=1, replica_groups=mesh['section'=2,'tensor'=4,'dp'=4] {'section','dp'}, use_global_device_ids=true, to_apply=%region_7.8 | all-reduce | flops 16 | bytes 128 | tf_op jit(solution)/shard_map/psum | solution.py:16
  126.2 8.2 %fusion.17 = f32[16,2,7168]{2,0,1:T(8,128)} fusion(bf16[2,512,7168]{2,1,0:T(8,128)(2,1)} %param.20, bf16[16,512]{1,0:T(8,128)(2,1)S(1)} %get-tuple-element.6, f32[512]{0:T(512)S(1)} %copy-done.3, f32[16]{0:T(128)S(1)} %add_rsqrt_fusion), kind=kOutput, calls=%fused_computation.32 | convolution fusion | flops 234913792 | bytes 15616064 | tf_op jit(solution)/shard_map/rd,kdf->rkf/dot_general | solution.py:112
  134.4 52.6 %all-reduce.7.cloned.1.call-done = f32[16,2,7168]{2,0,1:T(8,128)} async-done(((f32[16,2,7168]{2,0,1:T(8,128)}), f32[16,2,7168]{2,0,1:T(8,128)}) %all-reduce.7.cloned.1.call-update) | async-done | bytes 917520
  187.1 1.1 fusion.15
  188.2 8.6 %all-gather.1 = bf16[8,2,7168]{2,1,0:T(2,128)(2,1)S(1)} all-gather(bf16[1,2,7168]{2,1,0:T(2,128)(2,1)S(1)} %fusion.15), channel_id=1, replica_groups=mesh['section'=2,'tensor'=4,'dp'=4] {'section','dp'}, dimensions={0}, use_global_device_ids=true | all-gather | bytes 258048 | tf_op jit(solution)/shard_map/all_gather | solution.py:33
  196.8 4.1 %fusion.38 = f32[16,512]{1,0:T(8,128)S(1)} fusion(bf16[16,7168]{1,0:T(8,128)(2,1)S(1)} %reshape.132, bf16[7168,512]{1,0:T(8,128)(2,1)} %param.21), kind=kOutput, calls=%fused_computation.66 | convolution fusion | flops 117440512 | bytes 7602176 | tf_op jit(solution)/shard_map/dot_general | solution.py:32
  201.0 19.0 %psum.31 = f32[16,512]{1,0:T(8,128)S(1)} all-reduce(f32[16,512]{1,0:T(8,128)S(1)} %fusion.38), channel_id=1, replica_groups=mesh['section'=2,'tensor'=4,'dp'=4] {'tensor'}, use_global_device_ids=true, to_apply=%region_9.10 | all-reduce | flops 8192 | bytes 65536 | tf_op jit(solution)/shard_map/psum | solution.py:40
  220.0 0.6 fusion.14
  (28 shorter events, 0.8 us)
Async XLA Ops:
  6.5 16.1 %copy-start = (bf16[512,2560]{1,0:T(8,128)(2,1)S(1)}, bf16[512,2560]{1,0:T(8,128)(2,1)}, u32[]{:S(2)}) copy-start(bf16[512,2560]{1,0:T(8,128)(2,1)} %param.13) | copy-start | bytes 7864324
  6.5 69.9 %all-reduce.5.cloned.1.call-start = ((), (), s32[]{:S(2)}) async-start(), calls=%async_computation | async-start | bytes 327680
  24.6 162.5 %all-reduce.7.cloned.1.call-start = ((), (), s32[]{:S(2)}) async-start(), calls=%async_computation.1 | async-start | bytes 1835008
  77.3 5.2 %copy-start.1 = (bf16[2,2,4096,128]{3,2,1,0:T(8,128)(2,1)S(1)}, bf16[2,2,4096,128]{3,2,1,0:T(8,128)(2,1)}, u32[]{:S(2)}) copy-start(bf16[2,2,4096,128]{3,2,1,0:T(8,128)(2,1)} %param.16) | copy-start | bytes 12582916
  82.2 32.0 %copy-start.2 = (bf16[16,512]{1,0:T(8,128)(2,1)S(1)}, bf16[16,512]{1,0:T(8,128)(2,1)}, u32[]{:S(2)}) copy-start(bf16[16,512]{1,0:T(8,128)(2,1)} %param.11) | copy-start | bytes 49156
  82.2 44.0 %copy-start.3 = (f32[512]{0:T(512)S(1)}, f32[512]{0:T(512)}, u32[]{:S(2)}) copy-start(f32[512]{0:T(512)} %param.19) | copy-start | bytes 6148
Sparse Core Ops, SparseCore 0:
  24.7 51.6 all-reduce.4
  134.6 52.4 all-reduce.6
where the time goes:
time: 228 us; the launch traced here: 227 us
  waiting for transfers between devices  101 us (44%)
  blocking collectives  83.5 us (37%)
  matrix products  21.5 us (9%)
  between operations  14.2 us (6%)
  other arithmetic  4.91 us (2%)
  local copies, waits for them, and re-layouts  2.31 us (1%)
    unnamed x4, waiting for transfers between devices  101 us
    psum x2, blocking collectives, add_residual(): summed = lax.psum(partial_sum, 'tensor')  38 us
    psum x2, blocking collectives, normalize(): squares = lax.psum(jnp.sum(wide * wide, axis=1), ('section', 'dp'))  27 us
    all_gather x2, blocking collectives, project_rows(): lax.all_gather(row_block, ('section', 'dp'), axis=0, tiled=True)  18.6 us
    dot_general x1, matrix products, body(): jnp.einsum('rd,kdf->rkf', row_block, gate_up, preferred_element_type=jnp....  8.21 us
    dot_general x2, matrix products, project_rows(): jnp.dot(lax.all_gather(row_block, ('section', 'dp'), axis=0, tiled=True),...  6.09 us
  transfers between devices with their start and end apart: 2, of which 2 were waited for; matrix products, arithmetic and copies ran while one was open for 1% of the time, Pallas kernels for 0%

commit v1 on v0

--- a/solution.py
+++ b/solution.py
@@ -37,7 +37,7 @@
 
 
 def add_residual(base_rows, partial_sum):
-    summed = lax.psum(partial_sum, "tensor")
+    summed = jnp.sum(lax.all_gather(partial_sum, "tensor"), axis=0)
     return (base_rows.astype(jnp.float32) + summed).astype(jnp.bfloat16)
 
 

time: 228 us -> 220 us (0.965)
  blocking collectives: 83.5 us -> 72.5 us
  waiting for transfers between devices: 101 us -> 104 us
    psum x2 -> x0, blocking collectives: 38 us -> none  [add_residual(): summed = lax.psum(partial_sum, 'tensor')]
    all_gather x0 -> x2, blocking collectives: none -> 27 us  [add_residual(): summed = jnp.sum(lax.all_gather(partial_sum, 'tensor'), axis=0)]
    unnamed x4, waiting for transfers between devices: 101 us -> 104 us
where the time goes in v1:
time: 220 us; the launch traced here: 219 us
  waiting for transfers between devices  104 us (47%)
  blocking collectives  72.5 us (33%)
  matrix products  21.5 us (10%)
  between operations  14.2 us (6%)
  other arithmetic  4.93 us (2%)
  local copies, waits for them, and re-layouts  2.31 us (1%)
    unnamed x4, waiting for transfers between devices  104 us
    all_gather x2, blocking collectives, add_residual(): summed = jnp.sum(lax.all_gather(partial_sum, 'tensor'), axis=0)  27 us
    psum x2, blocking collectives, normalize(): squares = lax.psum(jnp.sum(wide * wide, axis=1), ('section', 'dp'))  27 us
    all_gather x2, blocking collectives, project_rows(): lax.all_gather(row_block, ('section', 'dp'), axis=0, tiled=True)  18.6 us
    dot_general x1, matrix products, body(): jnp.einsum('rd,kdf->rkf', row_block, gate_up, preferred_element_type=jnp....  8.21 us
    dot_general x2, matrix products, project_rows(): jnp.dot(lax.all_gather(row_block, ('section', 'dp'), axis=0, tiled=True),...  6.09 us
  transfers between devices with their start and end apart: 2, of which 2 were waited for; matrix products, arithmetic and copies ran while one was open for 1% of the time, Pallas kernels for 0%

profile of v1, /device:TPU:0, one launch (start us, length us, event | category | flops | bytes accessed | tf_op | source)
XLA Modules:
  0.0 219.2 jit_solution(9912678793520250653)
XLA Ops:
  6.5 1.0 fusion.7
  7.5 15.1 %psum.14 = f32[16]{0:T(128)S(1)} all-reduce(f32[16]{0:T(128)S(1)} %fusion.7), channel_id=1, replica_groups=mesh['section'=2,'tensor'=4,'dp'=4] {'section','dp'}, use_global_device_ids=true, to_apply=%region_1.0 | all-reduce | flops 16 | bytes 128 | tf_op jit(solution)/shard_map/psum | solution.py:16
  22.7 1.9 fusion.19
  24.6 0.7 convert_element_type.47
  25.3 0.7 iota_compare_fusion
  26.2 1.2 dynamic-slice
  28.1 48.3 %all-reduce.5.cloned.1.call-done = f32[16,2560]{1,0:T(8,128)} async-done(((f32[16,2560]{1,0:T(8,128)}), f32[16,2560]{1,0:T(8,128)}) %all-reduce.5.cloned.1.call-update) | async-done | bytes 163856
  76.4 0.9 constant_dynamic-slice_fusion
  77.3 0.9 convolution_bitcast_fusion
  78.5 0.2 fusion.29
  78.7 3.5 %fusion.36 = (f32[2,2,8]{2,1,0:T(2,128)S(1)}, f32[2,2,8,4096]{3,2,1,0:T(8,128)S(1)}) fusion(bf16[2,2,4096,128]{3,2,1,0:T(8,128)(2,1)} %param.15, bf16[2,2,8,64]{3,2,1,0:T(8,128)(2,1)S(1)} %get-tuple-element.8, bf16[2,2,8,64]{3,2,1,0:T(8,128)(2,1)S(1)} %get-tuple-element.7, pred[2,4096]{1,0:T(4,128)(4,1)S(1)} %iota_compare_fusion), kind=kOutput, calls=%fused_computation.64 | convolution fusion | flops 33964000 | bytes 4735104 | tf_op jit(solution)/shard_map/bgpd,bgld->bgpl/dot_general | solution.py:85
  82.3 0.2 fusion.2
  82.5 0.7 fusion.1
  83.3 10.0 %all-gather.2 = bf16[8,2,2048]{2,1,0:T(2,128)(2,1)S(1)} all-gather(bf16[1,2,2048]{2,1,0:T(2,128)(2,1)S(1)} %reshape.131), channel_id=1, replica_groups=mesh['section'=2,'tensor'=4,'dp'=4] {'section','dp'}, dimensions={0}, use_global_device_ids=true | all-gather | bytes 73728 | tf_op jit(solution)/shard_map/all_gather | solution.py:33
  93.3 2.0 fusion.37
  95.3 13.5 %all-gather = f32[64,512]{1,0:T(8,128)S(1)} all-gather(f32[16,512]{1,0:T(8,128)S(1)} %fusion.37), channel_id=2, replica_groups=mesh['section'=2,'tensor'=4,'dp'=4] {'tensor'}, dimensions={0}, use_global_device_ids=true | all-gather | bytes 163840 | tf_op jit(solution)/shard_map/all_gather | solution.py:40
  108.9 11.8 %psum.15 = f32[16]{0:T(128)S(1)} all-reduce(f32[16]{0:T(128)S(1)} %get-tuple-element.5), channel_id=1, replica_groups=mesh['section'=2,'tensor'=4,'dp'=4] {'section','dp'}, use_global_device_ids=true, to_apply=%region_7.8 | all-reduce | flops 16 | bytes 128 | tf_op jit(solution)/shard_map/psum | solution.py:16
  120.7 8.2 %fusion.17 = f32[16,2,7168]{2,0,1:T(8,128)} fusion(bf16[2,512,7168]{2,1,0:T(8,128)(2,1)} %param.20, bf16[16,512]{1,0:T(8,128)(2,1)S(1)} %get-tuple-element.6, f32[512]{0:T(512)S(1)} %copy-done.3, f32[16]{0:T(128)S(1)} %add_rsqrt_fusion), kind=kOutput, calls=%fused_computation.32 | convolution fusion | flops 234913792 | bytes 15616064 | tf_op jit(solution)/shard_map/rd,kdf->rkf/dot_general | solution.py:112
  129.0 55.4 %all-reduce.7.cloned.1.call-done = f32[16,2,7168]{2,0,1:T(8,128)} async-done(((f32[16,2,7168]{2,0,1:T(8,128)}), f32[16,2,7168]{2,0,1:T(8,128)}) %all-reduce.7.cloned.1.call-update) | async-done | bytes 917520
  184.4 1.1 fusion.15
  185.5 8.6 %all-gather.3 = bf16[8,2,7168]{2,1,0:T(2,128)(2,1)S(1)} all-gather(bf16[1,2,7168]{2,1,0:T(2,128)(2,1)S(1)} %fusion.15), channel_id=1, replica_groups=mesh['section'=2,'tensor'=4,'dp'=4] {'section','dp'}, dimensions={0}, use_global_device_ids=true | all-gather | bytes 258048 | tf_op jit(solution)/shard_map/all_gather | solution.py:33
  194.1 4.1 %fusion.38 = f32[16,512]{1,0:T(8,128)S(1)} fusion(bf16[16,7168]{1,0:T(8,128)(2,1)S(1)} %reshape.134, bf16[7168,512]{1,0:T(8,128)(2,1)} %param.21), kind=kOutput, calls=%fused_computation.66 | convolution fusion | flops 117440512 | bytes 7602176 | tf_op jit(solution)/shard_map/dot_general | solution.py:32
  198.3 13.5 %all-gather.1 = f32[64,512]{1,0:T(8,128)S(1)} all-gather(f32[16,512]{1,0:T(8,128)S(1)} %fusion.38), channel_id=3, replica_groups=mesh['section'=2,'tensor'=4,'dp'=4] {'tensor'}, dimensions={0}, use_global_device_ids=true | all-gather | bytes 163840 | tf_op jit(solution)/shard_map/all_gather | solution.py:40
  211.8 0.6 fusion.14
  (30 shorter events, 0.8 us)
Async XLA Ops:
  6.5 16.1 %copy-start = (bf16[512,2560]{1,0:T(8,128)(2,1)S(1)}, bf16[512,2560]{1,0:T(8,128)(2,1)}, u32[]{:S(2)}) copy-start(bf16[512,2560]{1,0:T(8,128)(2,1)} %param.13) | copy-start | bytes 7864324
  6.5 69.9 %all-reduce.5.cloned.1.call-start = ((), (), s32[]{:S(2)}) async-start(), calls=%async_computation | async-start | bytes 327680
  24.6 159.8 %all-reduce.7.cloned.1.call-start = ((), (), s32[]{:S(2)}) async-start(), calls=%async_computation.1 | async-start | bytes 1835008
  77.3 5.2 %copy-start.1 = (bf16[2,2,4096,128]{3,2,1,0:T(8,128)(2,1)S(1)}, bf16[2,2,4096,128]{3,2,1,0:T(8,128)(2,1)}, u32[]{:S(2)}) copy-start(bf16[2,2,4096,128]{3,2,1,0:T(8,128)(2,1)} %param.16) | copy-start | bytes 12582916
  82.2 26.5 %copy-start.2 = (bf16[16,512]{1,0:T(8,128)(2,1)S(1)}, bf16[16,512]{1,0:T(8,128)(2,1)}, u32[]{:S(2)}) copy-start(bf16[16,512]{1,0:T(8,128)(2,1)} %param.11) | copy-start | bytes 49156
  82.2 38.5 %copy-start.3 = (f32[512]{0:T(512)S(1)}, f32[512]{0:T(512)}, u32[]{:S(2)}) copy-start(f32[512]{0:T(512)} %param.19) | copy-start | bytes 6148
Sparse Core Ops, SparseCore 0:
  24.7 51.6 all-reduce.4
  129.1 55.2 all-reduce.6
